TPU v7x, 32 devices: a whole 2x2x4 slice. The times are simulated.
32 devices in a mesh: section: 2 (over core), node: 4 (over z), local: 4 (over y, x).
Axes of the slice: x: 2, y: 2, z: 4, core: 2. Of those that a mesh axis runs over, the one named last changes fastest.
Arguments:
- tokens: bfloat16 [2, 1024, 768], P(None, ('node', 'local')), may hold values from -18 to 18
- expert_ids: int32 [2, 2, 1024, 2], P('section', None, ('node', 'local')), may hold values from 0 to 15, as said below
- slots: int32 [2, 2, 1024, 2], P('section', None, ('node', 'local')), may hold values from -1 to 31, as said below
- gates: float32 [2, 2, 1024, 2], P('section', None, ('node', 'local')), may hold values from 0.2 to 1
- gain: float32 [2, 768], P('section'), may hold values from 0.5 to 1.5
- w_gate: bfloat16 [2, 16, 768, 3072], P('section', ('node', 'local')), may hold values from -0.21875 to 0.21875
- w_up: bfloat16 [2, 16, 768, 3072], P('section', ('node', 'local')), may hold values from -0.21875 to 0.21875
- w_down: bfloat16 [2, 16, 3072, 768], P('section', ('node', 'local')), may hold values from -0.109375 to 0.109375
Outputs:
- hidden: bfloat16 [2, 2, 1024, 768], P('section', None, ('node', 'local'))
Inputs may be any that keep to these rules, and one draw needn't show every extreme that they name: `expert_ids`: in each layer and micro-batch the two ids of a token differ, no expert is named by more than 256 tokens, and some expert is named by exactly 256. Expert e lies on node e // 4. Among one device's 64 tokens of a micro-batch and layer, the kept tokens that reach one node hold distinct slots below 32, and the two choices of a token on one node carry the same slot; -1 marks a dropped choice.
All inputs are finite; a program needn't handle non-finite values.
Results may differ from a plain program's by a relative error of at most 0.0085.
Values may be sent and summed in bfloat16 or wider, within the bound.
A program may use at most 64 MiB of HBM per device.

v0:
```python
import functools

import jax
import jax.numpy as jnp
from jax import lax
from jax.experimental import pallas as pl
from jax.experimental.pallas import tpu as pltpu
from jax.sharding import PartitionSpec as P

MESH = pl.DeviceIdType.MESH
LANES = 128
FF_CHUNKS = 3


def relay_kernel(
    sizes,
    tok_ref, ids_ref, slots_ref, gates_ref, gain_ref, wg_hbm, wu_hbm, wd_hbm,
    out_ref,
    held, packed, arrived, answer, parts, summed, back, hits, hits_t, meta_out, meta_in,
    pick, pick_t, pick_w, acc, wg, wu, wd,
    w_sem, meta_send, meta_recv, out_send, out_recv, fan_send, fan_recv,
    part_send, part_recv, back_send, back_recv, relay_send, relay_recv,
):
    n_sec, n_node, n_local, micro, toks, width, cap, limit = sizes
    n = n_node * n_local
    total = n * cap
    groups = total // LANES
    sec = lax.axis_index("section")
    node = lax.axis_index("node")
    local = lax.axis_index("local")
    me = node * n_local + local

    def device(p):
        return {"node": lax.div(p, n_local), "local": lax.rem(p, n_local)}

    def peers(body):
        lax.fori_loop(1, n, lambda i, c: (body(lax.rem(me + i, n)), c)[1], 0)

    barrier = pltpu.get_barrier_semaphore()
    peers(lambda p: pl.semaphore_signal(barrier, inc=1, device_id=device(p), device_id_type=MESH))
    for i in range(1, n_sec):
        pl.semaphore_signal(
            barrier, inc=1, device_id={"section": lax.rem(sec + i, n_sec)}, device_id_type=MESH
        )

    def weight_copies(c):
        chunk = wg.shape[2]
        cols = pl.ds(pl.multiple_of(c * chunk, chunk), chunk)
        return (
            pltpu.make_async_copy(wg_hbm.at[:, cols], wg.at[c], w_sem.at[0, c]),
            pltpu.make_async_copy(wu_hbm.at[:, cols], wu.at[c], w_sem.at[1, c]),
            pltpu.make_async_copy(wd_hbm.at[cols, :], wd.at[c], w_sem.at[2, c]),
        )

    for c in range(FF_CHUNKS):
        for copy in weight_copies(c):
            copy.start()

    def meta_copy(p):
        return pltpu.make_async_remote_copy(
            meta_out.at[p], meta_in.at[me], meta_send.at[p], meta_recv.at[me],
            device_id=device(p), device_id_type=MESH,
        )

    def out_copy(mb, j):
        return pltpu.make_async_remote_copy(
            packed.at[mb, j], arrived.at[mb, me], out_send.at[mb, j],
            out_recv.at[mb, me], device_id={"node": j}, device_id_type=MESH,
        )

    def fan_copy(mb, j, i):
        block = j * n_local + local
        return pltpu.make_async_remote_copy(
            arrived.at[mb, block], arrived.at[mb, block], fan_send.at[mb, j * n_local + i],
            fan_recv.at[mb, block], device_id={"local": i}, device_id_type=MESH,
        )

    def part_copy(mb, j, i):
        return pltpu.make_async_remote_copy(
            answer.at[mb, j * n_local + i], parts.at[mb, j * n_local + local],
            part_send.at[mb, j * n_local + i], part_recv.at[mb, j * n_local + local],
            device_id={"local": i}, device_id_type=MESH,
        )

    def back_copy(mb, j):
        return pltpu.make_async_remote_copy(
            summed.at[mb, j], back.at[mb, node], back_send.at[mb, j],
            back_recv.at[mb, node], device_id={"node": j}, device_id_type=MESH,
        )

    def nodes(body):
        lax.fori_loop(1, n_node, lambda i, c: (body(lax.rem(node + i, n_node)), c)[1], 0)

    def locals_(body):
        for i in range(1, n_local):
            body(lax.rem(local + i, n_local))

    def arrival(buffer, sem, p):
        return pltpu.make_async_remote_copy(
            buffer.at[p], buffer.at[p], sem.at[p], sem.at[p],
            device_id={"section": lax.rem(sec + 1, n_sec)}, device_id_type=MESH,
        )

    def relay_copy(mb):
        return pltpu.make_async_remote_copy(
            out_ref.at[mb], held.at[mb], relay_send.at[mb], relay_recv.at[mb],
            device_id={"section": lax.rem(sec + 1, n_sec)}, device_id_type=MESH,
        )

    slot_span = lax.broadcasted_iota(jnp.int32, (n_node * cap, toks), 0)
    exp_span = lax.broadcasted_iota(jnp.int32, (n, toks), 0)
    lane_span = lax.broadcasted_iota(jnp.int32, (LANES, toks), 0)
    row_span = lax.broadcasted_iota(jnp.int32, (n, micro * groups, LANES), 1)
    my_group = lax.div(me * cap, LANES)
    my_lane = lax.rem(me * cap, LANES)
    meta = jnp.zeros((n, micro * groups, LANES), jnp.float32)
    for mb in range(micro):
        hit = None
        weights = None
        for k in range(2):
            e = ids_ref[mb, k : k + 1, :]
            s = slots_ref[mb, k : k + 1, :]
            g = gates_ref[mb, k : k + 1, :]
            pos = jnp.where(s >= 0, lax.div(e, jnp.full_like(e, n_local)) * cap + s, -1)
            this = jnp.where(pos == slot_span, 1.0, 0.0)
            hit = this if hit is None else jnp.maximum(hit, this)
            lane = jnp.where(s >= 0, my_lane + s, -1)
            part = lax.dot_general(
                jnp.where(e == exp_span, g, 0.0),
                jnp.where(lane == lane_span, 1.0, 0.0),
                (((1,), (1,)), ((), ())),
                precision=lax.Precision.HIGHEST,
                preferred_element_type=jnp.float32,
            )
            weights = part if weights is None else weights + part
        hits[mb] = hit.astype(jnp.bfloat16)
        hits_t[mb] = hit.T.astype(jnp.bfloat16)
        meta = meta + jnp.where(row_span == mb * groups + my_group, weights[:, None, :], 0.0)
    meta_out[...] = meta
    meta_in[me] = meta_out[me]

    def pack(mb, h):
        floats = h.astype(jnp.float32)
        mean_square = jnp.mean(floats * floats, axis=-1, keepdims=True)
        normed = (floats * lax.rsqrt(mean_square + 1e-05) * gain_ref[...]).astype(jnp.bfloat16)
        rows = jnp.dot(hits[mb], normed, preferred_element_type=jnp.float32)
        for j in range(n_node):
            packed[mb, j] = rows[j * cap : (j + 1) * cap].astype(jnp.bfloat16)
        arrived[mb, me] = packed[mb, node]

    def dispatch(mb):
        nodes(lambda j: out_copy(mb, j).start())
        locals_(lambda i: fan_copy(mb, node, i).start())

    def hand_on(mb):
        def step(i, carry):
            j = lax.rem(node + n_node - i, n_node)
            arrival(arrived.at[mb], out_recv.at[mb], j * n_local + local).wait_recv()
            locals_(lambda k: fan_copy(mb, j, k).start())
            return carry

        lax.fori_loop(1, n_node, step, 0)

    @pl.when(sec == 0)
    def _():
        held[...] = tok_ref[...]
        pack(0, held[0])

    pl.semaphore_wait(barrier, n - 1 + n_sec - 1)
    peers(lambda p: meta_copy(p).start())

    @pl.when(sec == 0)
    def _():
        dispatch(0)
        for mb in range(1, micro):
            pack(mb, held[mb])
            dispatch(mb)
        for mb in range(micro):
            hand_on(mb)

    peers(lambda p: arrival(meta_in, meta_recv, p).wait_recv())
    meta = jnp.sum(meta_in[...], axis=0)
    upto = lax.broadcasted_iota(jnp.int32, (total, total), 0) <= lax.broadcasted_iota(
        jnp.int32, (total, total), 1
    )
    upto = jnp.where(upto, 1.0, 0.0).astype(jnp.bfloat16)
    spot = lax.broadcasted_iota(jnp.int32, (limit, total), 0).astype(jnp.float32)
    for mb in range(micro):
        w_row = jnp.concatenate(
            [meta[mb * groups + g : mb * groups + g + 1] for g in range(groups)], axis=1
        )
        w_rows = jnp.broadcast_to(w_row, (8, total))
        chosen = jnp.where(w_rows > 0.0, 1.0, 0.0)
        rank = jnp.dot(chosen.astype(jnp.bfloat16), upto, preferred_element_type=jnp.float32)
        rank = jnp.where(w_rows > 0.0, rank - 1.0, -1.0)
        is_at = spot == jnp.broadcast_to(rank[0:1], (limit, total))
        place = jnp.where(is_at, 1.0, 0.0)
        pick[mb] = place.astype(jnp.bfloat16)
        pick_t[mb] = place.T.astype(jnp.bfloat16)
        pick_w[mb] = jnp.sum(
            jnp.where(is_at, jnp.broadcast_to(w_row, (limit, total)), 0.0), axis=1, keepdims=True
        )

    @pl.when(sec > 0)
    def _():
        for mb in range(micro):
            relay_copy(mb).wait_recv()
            pack(mb, held[mb])
            dispatch(mb)
            hand_on(mb)

    def flat(blocks):
        if cap % 16:
            return blocks.astype(jnp.float32).reshape(-1, width).astype(jnp.bfloat16)
        return blocks.reshape(-1, width)

    for mb in range(micro):

        def wait_fan(j, carry):
            locals_(
                lambda i: arrival(arrived.at[mb], fan_recv.at[mb], j * n_local + i).wait_recv()
            )
            return carry

        lax.fori_loop(0, n_node, wait_fan, 0)
        rows = flat(arrived[mb])
        x = jnp.dot(pick[mb], rows, preferred_element_type=jnp.float32).astype(jnp.bfloat16)
        acc[...] = jnp.zeros_like(acc)

        def chunk_step(c, carry):
            if mb == 0:
                for copy in weight_copies(c):
                    copy.wait()
            gate = jnp.dot(x, wg[c], preferred_element_type=jnp.float32)
            up = jnp.dot(x, wu[c], preferred_element_type=jnp.float32)
            inner = (jax.nn.gelu(gate, approximate=True) * up).astype(jnp.bfloat16)
            acc[...] += jnp.dot(inner, wd[c], preferred_element_type=jnp.float32)
            return carry

        lax.fori_loop(0, FF_CHUNKS, chunk_step, 0)
        scaled = (pick_w[mb] * acc[...]).astype(jnp.bfloat16)
        spread = jnp.dot(pick_t[mb], scaled, preferred_element_type=jnp.float32)
        answer[mb] = spread.reshape(n, cap, width).astype(jnp.bfloat16)
        nodes(lambda j: locals_(lambda i: part_copy(mb, j, i).start()))
        locals_(lambda i: part_copy(mb, node, i).start())

    for mb in range(micro):

        def add_up(j):
            rows = answer[mb, j * n_local + local].astype(jnp.float32)
            locals_(
                lambda i: arrival(parts.at[mb], part_recv.at[mb], j * n_local + i).wait_recv()
            )
            for i in range(1, n_local):
                block = j * n_local + lax.rem(local + i, n_local)
                rows = rows + parts[mb, block].astype(jnp.float32)
            return rows.astype(jnp.bfloat16)

        def send_back(j):
            summed[mb, j] = add_up(j)
            back_copy(mb, j).start()

        nodes(send_back)
        back[mb, node] = add_up(node)
        nodes(lambda j: arrival(back.at[mb], back_recv.at[mb], j).wait_recv())
        mixed = jnp.dot(hits_t[mb], flat(back[mb]), preferred_element_type=jnp.float32)
        out_ref[mb] = (held[mb].astype(jnp.float32) + mixed).astype(jnp.bfloat16)

        @pl.when(sec < n_sec - 1)
        def _():
            relay_copy(mb).start()

    peers(lambda p: meta_copy(p).wait_send())
    for mb in range(micro):

        def settle(j):
            locals_(lambda i: fan_copy(mb, j, i).wait_send())
            locals_(lambda i: part_copy(mb, j, i).wait_send())

        nodes(lambda j: (out_copy(mb, j).wait_send(), back_copy(mb, j).wait_send()))
        nodes(settle)
        settle(node)

    @pl.when(sec < n_sec - 1)
    def _():
        for mb in range(micro):
            relay_copy(mb).wait_send()


def solution(mesh):
    n_sec, n_node, n_local = mesh.shape["section"], mesh.shape["node"], mesh.shape["local"]
    n = n_node * n_local

    def on_device(tokens, expert_ids, slots, gates, gain, w_gate, w_up, w_down):
        micro, toks, width = tokens.shape
        hidden = w_gate.shape[3]
        cap = 2 * toks // n_node
        limit = 4 * toks
        total = n * cap
        chunk = hidden // FF_CHUNKS
        sizes = (n_sec, n_node, n_local, micro, toks, width, cap, limit)
        half, full = jnp.bfloat16, jnp.float32
        vmem = pl.BlockSpec(memory_space=pltpu.VMEM)
        hbm = pl.BlockSpec(memory_space=pl.ANY)
        dma = pltpu.SemaphoreType.DMA
        rows = micro * total // LANES
        out = pl.pallas_call(
            functools.partial(relay_kernel, sizes),
            out_shape=jax.ShapeDtypeStruct((micro, toks, width), half),
            in_specs=[vmem] * 5 + [hbm] * 3,
            out_specs=vmem,
            scratch_shapes=[
                pltpu.VMEM((micro, toks, width), half),
                pltpu.VMEM((micro, n_node, cap, width), half),
                pltpu.VMEM((micro, n, cap, width), half),
                pltpu.VMEM((micro, n, cap, width), half),
                pltpu.VMEM((micro, n, cap, width), half),
                pltpu.VMEM((micro, n_node, cap, width), half),
                pltpu.VMEM((micro, n_node, cap, width), half),
                pltpu.VMEM((micro, n_node * cap, toks), half),
                pltpu.VMEM((micro, toks, n_node * cap), half),
                pltpu.VMEM((n, rows, LANES), full),
                pltpu.VMEM((n, rows, LANES), full),
                pltpu.VMEM((micro, limit, total), half),
                pltpu.VMEM((micro, total, limit), half),
                pltpu.VMEM((micro, limit, 1), full),
                pltpu.VMEM((limit, width), full),
                pltpu.VMEM((FF_CHUNKS, width, chunk), half),
                pltpu.VMEM((FF_CHUNKS, width, chunk), half),
                pltpu.VMEM((FF_CHUNKS, chunk, width), half),
                dma((3, FF_CHUNKS)),
                dma((n,)), dma((n,)),
                dma((micro, n_node)), dma((micro, n)),
                dma((micro, n)), dma((micro, n)),
                dma((micro, n)), dma((micro, n)),
                dma((micro, n_node)), dma((micro, n_node)),
                dma((micro,)), dma((micro,)),
            ],
            compiler_params=pltpu.CompilerParams(collective_id=0, has_side_effects=True),
        )(
            tokens, *(jnp.swapaxes(a[0], 1, 2) for a in (expert_ids, slots, gates)), gain,
            w_gate[0, 0], w_up[0, 0], w_down[0, 0],
        )
        return out[None]

    placed = (
        P(None, ("node", "local"), None),
        P("section", None, ("node", "local"), None),
        P("section", None, ("node", "local"), None),
        P("section", None, ("node", "local"), None),
        P("section", None),
        P("section", ("node", "local"), None, None),
        P("section", ("node", "local"), None, None),
        P("section", ("node", "local"), None, None),
    )
    return jax.shard_map(
        on_device,
        mesh=mesh,
        in_specs=placed,
        out_specs=P("section", None, ("node", "local"), None),
        check_vma=False,
    )
```

profile of v0, /device:TPU:1, one launch (start us, length us, event | category | flops | bytes accessed | tf_op | source)
XLA Modules:
  0.0 69.3 jit_solution(221946645042806553)
XLA Ops:
  0.0 67.7 %shard_map.82 = bf16[2,64,768]{2,1,0:T(8,128)(2,1)} custom-call(bf16[2,64,768]{2,1,0:T(8,128)(2,1)} %tok_ref.1, s32[2,2,64]{2,1,0:T(2,128)} %bitcast.17, s32[2,2,64]{2,1,0:T(2,128)} %bitcast.18, f32[2,2,64]{2,1,0:T(2,128)} %bitcast.19, f32[1,768]{1,0:T(1,128)} %gain_ref.1, bf16[768,3072]{1,0:T(8,128)(2,1)} %bitcast.13, bf16[768,3072]{1,0:T(8,128)(2,1)} %bitcast.14, ...), custom_call_target="tpu_custom_call" | custom-call | tf_op jit(solution)/shard_map/pallas_call | solution.py:307
  67.7 1.6 %copy.10 = bf16[1,2,64,768]{3,2,1,0:T(8,128)(2,1)} copy(bf16[1,2,64,768]{3,2,1,0:T(8,128)(2,1)} %bitcast.16) | data formatting | bytes 393216
where the time goes:
time: 69.4 us; the launch traced here: 69.3 us
  Pallas kernels  67.7 us (98%)
  local copies, waits for them, and re-layouts  1.62 us (2%)
    pallas_call x1, Pallas kernels, on_device(): pl.pallas_call(functools.partial(relay_kernel, sizes), out_shape=jax.Shap...  67.7 us
    unnamed x1, local copies, waits for them, and re-layouts  1.62 us

commit v1 on v0

v1 whole, which is shorter than its diff:
```python
import functools

import jax
import jax.numpy as jnp
from jax import lax
from jax.experimental import pallas as pl
from jax.experimental.pallas import tpu as pltpu
from jax.sharding import PartitionSpec as P

MESH = pl.DeviceIdType.MESH
LANES = 128
NS = jax.named_scope


def relay_kernel(
    sizes,
    tok_hbm, ids_hbm, slots_hbm, gates_hbm, gain_hbm, wg_hbm, wu_hbm, wd_hbm,
    out_ref,
    tok, ids, slots, gates, gain, held, packed, relay, arrived, answer, parts, summed, back,
    hits, hits_t, first_t, meta_out, meta_z, meta_in, pick, pick_t, pick_w,
    xs, inner, scaled, wg, wu, wd,
    in_sem, w_sem, first_send, first_recv, mz_send, mz_recv, mo_send, mo_recv, mf_send, mf_recv,
    z_send, z_recv, own_send, own_recv, fan_send, fan_recv, part_send, part_recv,
    back_send, back_recv, relay_send, relay_recv,
):
    n_node, n_local, micro, toks, width, cap, limit, chunks, ff_chunks = sizes
    n = n_node * n_local
    total = n * cap
    cw = width // chunks
    fw = inner.shape[1] // ff_chunks
    half = jnp.bfloat16
    sec = lax.axis_index("section")
    node = lax.axis_index("node")
    local = lax.axis_index("local")
    me = local * n_node + node

    def near(k):
        if n_node != 4:
            return lax.rem(node + k, n_node)
        j = jnp.int32(0)
        for z in range(n_node):
            order = sorted((p for p in range(n_node) if p != z), key=lambda p: abs(p - z))
            j = jnp.where(node == z, order[k - 1], j)
        return j

    others = [near(k) for k in range(1, n_node)]
    plane = [lax.rem(local + i, n_local) for i in range(1, n_local)]

    def remote(src, dst, send, recv, **to):
        return pltpu.make_async_remote_copy(
            src, dst, send, recv, device_id=to, device_id_type=MESH
        )

    def got(ref, sem):
        remote(ref, ref, sem, sem, section=1 - sec).wait_recv()

    def sent(ref, sem):
        remote(ref, ref, sem, sem, section=1 - sec).wait_send()

    barrier = pltpu.get_barrier_semaphore()

    def greet(**to):
        pl.semaphore_signal(barrier, inc=1, device_id=to, device_id_type=MESH)

    greet(section=1 - sec)
    for j in others:
        greet(section=1 - sec, node=j)
    for i in plane:
        greet(local=i)
        greet(section=1 - sec, local=i)

    @pl.when(sec == 1)
    def _():
        for j in others:
            greet(node=j)

    loads = [
        pltpu.make_async_copy(src, dst, in_sem.at[i])
        for i, (src, dst) in enumerate(
            ((ids_hbm, ids), (slots_hbm, slots), (gates_hbm, gates), (tok_hbm, tok), (gain_hbm, gain))
        )
    ]
    for load in loads:
        load.start()
    weights_in = [
        pltpu.make_async_copy(src, dst, w_sem.at[i])
        for i, (src, dst) in enumerate(((wg_hbm, wg), (wu_hbm, wu), (wd_hbm, wd)))
    ]
    for load in loads:
        load.wait()
    for copy in weights_in:
        copy.start()

    slot_span = lax.broadcasted_iota(jnp.int32, (n_node * cap, toks), 0)
    for mb in range(micro):
        hit = None
        for k in range(2):
            e = ids[mb, k : k + 1, :]
            s = slots[mb, k : k + 1, :]
            pos = jnp.where(s >= 0, lax.div(e, jnp.full_like(e, n_local)) * cap + s, -1)
            this = jnp.where(pos == slot_span, 1.0, 0.0)
            hit = this if hit is None else jnp.maximum(hit, this)
        hits[mb] = hit.astype(half)
        hits_t[mb] = hit.T.astype(half)

    def note_weights():
        exp_span = lax.broadcasted_iota(jnp.int32, (n, toks), 0)
        lane_span = lax.broadcasted_iota(jnp.int32, (LANES, toks), 0)
        my_lane = lax.rem(me * cap, LANES)
        for mb in range(micro):
            named = []
            lanes = []
            for k in range(2):
                e = ids[mb, k : k + 1, :]
                s = slots[mb, k : k + 1, :]
                lane = jnp.where(s >= 0, my_lane + s, -1)
                named.append(jnp.where(e == exp_span, gates[mb, k : k + 1, :], 0.0))
                lanes.append(jnp.where(lane == lane_span, 1.0, 0.0))
            weights = lax.dot_general(
                jnp.concatenate(named, axis=1),
                jnp.concatenate(lanes, axis=1),
                (((1,), (1,)), ((), ())),
                precision=lax.Precision.HIGHEST,
                preferred_element_type=jnp.float32,
            )
            for j in range(n_node):
                meta_out[j, mb * n_local : (mb + 1) * n_local] = weights[
                    j * n_local : (j + 1) * n_local
                ]
        meta_in[me] = meta_out[node]

    def pack(mb, h):
        floats = h.astype(jnp.float32)
        mean_square = jnp.mean(floats * floats, axis=-1, keepdims=True)
        normed = (floats * lax.rsqrt(mean_square + 1e-05) * gain[...]).astype(half)
        rows = jnp.dot(hits[mb], normed, preferred_element_type=jnp.float32)
        for j in range(n_node):
            packed[mb, j] = rows[j * cap : (j + 1) * cap].astype(half)
        arrived[mb, local, node] = packed[mb, node]

    def own_fan(mb, recv):
        for i in plane:
            remote(
                packed.at[mb, node], arrived.at[mb, local, node], own_send.at[mb], recv, local=i
            ).start()

    def flat(blocks):
        if cap % 16:
            blocks = blocks.astype(jnp.float32)
        return blocks.reshape(-1, blocks.shape[-1]).astype(half)

    def places():
        upto = lax.broadcasted_iota(jnp.int32, (total, total), 0) <= lax.broadcasted_iota(
            jnp.int32, (total, total), 1
        )
        upto = jnp.where(upto, 1.0, 0.0).astype(half)
        spot = lax.broadcasted_iota(jnp.int32, (limit, total), 0).astype(jnp.float32)
        per_group = LANES // cap
        for mb in range(micro):
            mine = pl.ds(mb * n_local + local, 1)
            w_row = jnp.concatenate(
                [
                    sum(meta_in[g * per_group + b, mine, :] for b in range(per_group))
                    for g in range(total // LANES)
                ],
                axis=1,
            )
            w_rows = jnp.broadcast_to(w_row, (8, total))
            chosen = jnp.where(w_rows > 0.0, 1.0, 0.0)
            rank = jnp.dot(chosen.astype(half), upto, preferred_element_type=jnp.float32)
            rank = jnp.where(w_rows > 0.0, rank - 1.0, -1.0)
            is_at = spot == jnp.broadcast_to(rank[0:1], (limit, total))
            place = jnp.where(is_at, 1.0, 0.0)
            pick[mb] = place.astype(half)
            pick_t[mb] = place.T.astype(half)
            pick_w[mb] = jnp.sum(
                jnp.where(is_at, jnp.broadcast_to(w_row, (limit, total)), 0.0),
                axis=1, keepdims=True,
            )

    def hand_second(mb):
        for j in others:
            block = arrived.at[mb, local, j]
            got(block, z_recv.at[1, mb, j])
            for i in plane:
                remote(block, block, fan_send.at[1, mb], fan_recv.at[mb], local=i).start()

    def expert(mb, carry):
        @pl.when(sec == 0)
        def _():
            with NS("fan"):
                got(arrived.at[mb, pl.ds(0, n_local - 1), 0], own_recv.at[mb])
                got(arrived.at[mb, :, pl.ds(0, n_node - 1)], fan_recv.at[mb])

        @pl.when(sec == 1)
        def _():
            with NS("fan"):
                got(arrived.at[mb, pl.ds(0, n_local - 1)], fan_recv.at[mb])

        with NS("pick"):
            xs[...] = jnp.dot(
                pick[mb], flat(arrived[mb]), preferred_element_type=jnp.float32
            ).astype(half)

        @pl.when(mb == 0)
        def _():
            for copy in weights_in:
                copy.wait()

        with NS("up"):
            for f in range(ff_chunks):
                cols = slice(f * fw, (f + 1) * fw)
                x = xs[...]
                gate = jnp.dot(x, wg[:, cols], preferred_element_type=jnp.float32)
                up = jnp.dot(x, wu[:, cols], preferred_element_type=jnp.float32)
                inner[:, cols] = (jax.nn.gelu(gate, approximate=True) * up).astype(half)
                if f == ff_chunks // 3 - 1:

                    @pl.when(jnp.logical_and(sec == 1, mb + 1 < micro))
                    def _():
                        hand_second(mb + 1)

        def down(c):
            acc = jnp.dot(
                inner[...], wd[:, c * cw : (c + 1) * cw], preferred_element_type=jnp.float32
            )
            scaled[c] = (pick_w[mb] * acc).astype(half)

        with NS("down"):
            down(0)
            for c in range(chunks):
                if c + 1 < chunks:
                    down(c + 1)
                spread = jnp.dot(pick_t[mb], scaled[c], preferred_element_type=jnp.float32)
                answer[mb, c] = spread.reshape(n_local, n_node, cap, cw).astype(half)
                for i in plane:
                    remote(
                        answer.at[mb, c, i], parts.at[sec, mb, c, local],
                        part_send.at[mb], part_recv.at[sec, mb, c], section=1, local=i,
                    ).start()

        @pl.when(sec == 0)
        def _():
            for c in range(chunks):
                remote(
                    answer.at[mb, c, local], parts.at[0, mb, c, local],
                    part_send.at[mb], part_recv.at[0, mb, c], section=1,
                ).start()

        return carry

    def collect(layer, mb, c):
        if layer == 0:
            got(parts.at[0, mb, c], part_recv.at[0, mb, c])
            rows = sum(parts[0, mb, c, i].astype(jnp.float32) for i in range(n_local))
        else:
            got(parts.at[1, mb, c, pl.ds(0, n_local - 1)], part_recv.at[1, mb, c])
            rows = answer[mb, c, local].astype(jnp.float32)
            for i in plane:
                rows = rows + parts[1, mb, c, i].astype(jnp.float32)
        summed[layer, mb, c] = rows.astype(half)
        for j in others:
            remote(
                summed.at[layer, mb, c, j], back.at[layer, mb, c, node],
                back_send.at[layer, mb], back_recv.at[layer, mb, c], node=j,
            ).start()
        back[layer, mb, c, node] = summed[layer, mb, c, node]

    def combine(layer, mb, base, where):
        for c in range(chunks):
            got(back.at[layer, mb, c, pl.ds(0, n_node - 1)], back_recv.at[layer, mb, c])
            mixed = jnp.dot(
                (first_t if layer == 0 else hits_t)[mb], flat(back[layer, mb, c]),
                preferred_element_type=jnp.float32,
            )
            cols = slice(c * cw, (c + 1) * cw)
            where[mb, :, cols] = (base[mb, :, cols].astype(jnp.float32) + mixed).astype(half)

    @pl.when(sec == 0)
    def _():
        pack(0, tok[0])
        with NS("barrier"):
            pl.semaphore_wait(barrier, 1 + n_node - 1 + 2 * (n_local - 1))

        def z_out(mb):
            for j in others:
                remote(
                    packed.at[mb, j], relay.at[mb, node], z_send.at[mb],
                    z_recv.at[0, mb, node], section=1, node=j,
                ).start()

        z_out(0)
        own_fan(0, own_recv.at[0])
        note_weights()
        for j in others:
            remote(
                meta_out.at[j], meta_z.at[node], mz_send, mz_recv.at[0, node], section=1, node=j
            ).start()
        for i in plane:
            remote(meta_out.at[node], meta_in.at[me], mo_send, mo_recv, local=i).start()
        for mb in range(1, micro):
            pack(mb, tok[mb])
            z_out(mb)
        remote(hits_t, first_t, first_send, first_recv, section=1).start()
        with NS("metawait"):
            got(meta_in.at[pl.ds(0, n_local - 1)], mo_recv)
            got(meta_in.at[pl.ds(0, (n_node - 1) * n_local)], mf_recv)
        places()
        for mb in range(1, micro):
            own_fan(mb, own_recv.at[mb])

    @pl.when(sec == 1)
    def _():
        with NS("barrier"):
            pl.semaphore_wait(barrier, 1 + 2 * (n_node - 1) + 2 * (n_local - 1))

        def hand_first(mb, nodes):
            for j in nodes:
                got(relay.at[mb, j], z_recv.at[0, mb, j])
                for i in plane + [local]:
                    remote(
                        relay.at[mb, j], arrived.at[mb, local, j],
                        fan_send.at[0, mb], fan_recv.at[mb], section=0, local=i,
                    ).start()

        note_weights()
        with NS("hand0"):
            hand_first(0, others[:-1])
        with NS("relaymeta"):
            for j in others:
                got(meta_z.at[j], mz_recv.at[0, j])
                for i in plane + [local]:
                    remote(
                        meta_z.at[j], meta_in.at[local * n_node + j], mf_send.at[0], mf_recv,
                        section=0, local=i,
                    ).start()
        with NS("hand0b"):
            hand_first(0, others[-1:])
        for j in others:
            remote(
                meta_out.at[j], meta_in.at[me], mz_send, mz_recv.at[1, node], node=j
            ).start()
        for i in plane:
            remote(meta_out.at[node], meta_in.at[me], mo_send, mo_recv, local=i).start()
        for mb in range(1, micro):
            with NS(f"hand{mb}"):
                hand_first(mb, others)
        with NS("handm"):
            for j in others:
                block = meta_in.at[local * n_node + j]
                got(block, mz_recv.at[1, j])
                for i in plane:
                    remote(block, block, mf_send.at[1], mf_recv, local=i).start()
        with NS("metawait"):
            got(meta_in.at[pl.ds(0, n_local - 1)], mo_recv)
            got(meta_in.at[pl.ds(0, (n_node - 1) * (n_local - 1))], mf_recv)
            got(first_t, first_recv)
        places()

        def dispatch(mb):
            pack(mb, held[mb])
            for j in others:
                remote(
                    packed.at[mb, j], arrived.at[mb, local, node], z_send.at[mb],
                    z_recv.at[1, mb, node], node=j,
                ).start()
            own_fan(mb, fan_recv.at[mb])
            remote(
                held.at[mb], held.at[mb], relay_send.at[mb], relay_recv.at[mb], section=0
            ).start()

        with NS("collect00"):
            for c in range(chunks):
                collect(0, 0, c)
        with NS("combine00"):
            combine(0, 0, tok, held)
        dispatch(0)
        for mb in range(1, micro):
            for c in range(chunks):
                with NS(f"collect0{mb}{c}"):
                    collect(0, mb, c)
            if mb == 1:
                with NS("second0"):
                    hand_second(0)
            with NS(f"combine0{mb}"):
                combine(0, mb, tok, held)
            dispatch(mb)

    lax.fori_loop(0, micro, expert, 0)

    @pl.when(sec == 0)
    def _():
        for mb in range(micro):
            with NS(f"relaywait{mb}"):
                got(held.at[mb], relay_recv.at[mb])
            out_ref[mb] = held[mb]
        sent(meta_out.at[pl.ds(0, n_node - 1)], mz_send)
        sent(meta_in.at[pl.ds(0, n_local - 1)], mo_send)
        sent(hits_t, first_send)
        for mb in range(micro):
            sent(packed.at[mb, pl.ds(0, n_node - 1)], z_send.at[mb])
            sent(arrived.at[mb, pl.ds(0, n_local - 1), 0], own_send.at[mb])
            sent(answer.at[mb], part_send.at[mb])

    @pl.when(sec == 1)
    def _():
        for mb in range(micro):
            with NS(f"collect1{mb}"):
                for c in range(chunks):
                    collect(1, mb, c)
        for mb in range(micro):
            with NS(f"combine1{mb}"):
                combine(1, mb, held, out_ref)
        with NS("settle"):
            sent(meta_out.at[pl.ds(0, n_node - 1)], mz_send)
            sent(meta_in.at[pl.ds(0, n_local - 1)], mo_send)
            sent(meta_in.at[pl.ds(0, (n_node - 1) * n_local)], mf_send.at[0])
            sent(meta_in.at[pl.ds(0, (n_node - 1) * (n_local - 1))], mf_send.at[1])
            for mb in range(micro):
                sent(packed.at[mb, pl.ds(0, n_node - 1)], z_send.at[mb])
                sent(arrived.at[mb, pl.ds(0, n_local - 1), 0], own_send.at[mb])
                sent(arrived.at[mb, :, pl.ds(0, n_node - 1)], fan_send.at[0, mb])
                sent(arrived.at[mb, pl.ds(0, n_local - 1), pl.ds(0, n_node - 1)], fan_send.at[1, mb])
                sent(answer.at[mb, :, pl.ds(0, n_local - 1)], part_send.at[mb])
                for layer in range(2):
                    sent(summed.at[layer, mb, :, pl.ds(0, n_node - 1)], back_send.at[layer, mb])
                sent(held.at[mb], relay_send.at[mb])


def solution(mesh):
    n_sec, n_node, n_local = mesh.shape["section"], mesh.shape["node"], mesh.shape["local"]
    n = n_node * n_local
    assert n_sec == 2

    def on_device(tokens, expert_ids, slots, gates, gain, w_gate, w_up, w_down):
        micro, toks, width = tokens.shape
        hidden = w_gate.shape[3]
        cap = 2 * toks // n_node
        limit = 4 * toks
        total = n * cap
        chunks = width // 256
        ff_chunks = hidden // 512
        cw = width // chunks
        sizes = (n_node, n_local, micro, toks, width, cap, limit, chunks, ff_chunks)
        half, full = jnp.bfloat16, jnp.float32
        vmem = pl.BlockSpec(memory_space=pltpu.VMEM)
        hbm = pl.BlockSpec(memory_space=pl.ANY)
        dma = pltpu.SemaphoreType.DMA
        mem = pltpu.VMEM
        out = pl.pallas_call(
            functools.partial(relay_kernel, sizes),
            out_shape=jax.ShapeDtypeStruct((micro, toks, width), half),
            in_specs=[hbm] * 8,
            out_specs=vmem,
            scratch_shapes=[
                mem((micro, toks, width), half),
                mem((micro, 2, toks), jnp.int32),
                mem((micro, 2, toks), jnp.int32),
                mem((micro, 2, toks), full),
                mem((1, width), full),
                mem((micro, toks, width), half),
                mem((micro, n_node, cap, width), half),
                mem((micro, n_node, cap, width), half),
                mem((micro, n_local, n_node, cap, width), half),
                mem((micro, chunks, n_local, n_node, cap, cw), half),
                mem((2, micro, chunks, n_local, n_node, cap, cw), half),
                mem((2, micro, chunks, n_node, cap, cw), half),
                mem((2, micro, chunks, n_node, cap, cw), half),
                mem((micro, n_node * cap, toks), half),
                mem((micro, toks, n_node * cap), half),
                mem((micro, toks, n_node * cap), half),
                mem((n_node, micro * n_local, LANES), full),
                mem((n_node, micro * n_local, LANES), full),
                mem((n, micro * n_local, LANES), full),
                mem((micro, limit, total), half),
                mem((micro, total, limit), half),
                mem((micro, limit, 1), full),
                mem((limit, width), half),
                mem((limit, hidden), half),
                mem((chunks, limit, cw), half),
                mem((width, hidden), half),
                mem((width, hidden), half),
                mem((hidden, width), half),
                dma((5,)), dma((3,)),
                dma(()), dma(()),
                dma(()), dma((2, n_node)), dma(()), dma(()), dma((2,)), dma(()),
                dma((micro,)), dma((2, micro, n_node)), dma((micro,)), dma((micro,)),
                dma((2, micro)), dma((micro,)),
                dma((micro,)), dma((2, micro, chunks)),
                dma((2, micro)), dma((2, micro, chunks)),
                dma((micro,)), dma((micro,)),
            ],
            compiler_params=pltpu.CompilerParams(collective_id=0, has_side_effects=True),
        )(
            tokens, *(jnp.swapaxes(a[0], 1, 2) for a in (expert_ids, slots, gates)), gain,
            w_gate[0, 0], w_up[0, 0], w_down[0, 0],
        )
        return out[None]

    placed = (
        P(None, ("node", "local"), None),
        P("section", None, ("node", "local"), None),
        P("section", None, ("node", "local"), None),
        P("section", None, ("node", "local"), None),
        P("section", None),
        P("section", ("node", "local"), None, None),
        P("section", ("node", "local"), None, None),
        P("section", ("node", "local"), None, None),
    )
    return jax.shard_map(
        on_device,
        mesh=mesh,
        in_specs=placed,
        out_specs=P("section", None, ("node", "local"), None),
        check_vma=False,
    )
```

time: 69.4 us -> 61.1 us (0.88)
  Pallas kernels: 67.7 us -> 59.3 us
    pallas_call x1, Pallas kernels: 67.7 us -> 59.3 us  [on_device(): pl.pallas_call(functools.partial(relay_kernel, sizes), out_shape=jax.Shap...]
where the time goes in v1:
time: 61.1 us; the launch traced here: 61 us
  Pallas kernels  59.3 us (97%)
  local copies, waits for them, and re-layouts  1.62 us (3%)
    pallas_call x1, Pallas kernels, on_device(): pl.pallas_call(functools.partial(relay_kernel, sizes), out_shape=jax.Shap...  59.3 us
    unnamed x1, local copies, waits for them, and re-layouts  1.62 us

profile of v1, /device:TPU:1, one launch (start us, length us, event | category | flops | bytes accessed | tf_op | source)
XLA Modules:
  0.0 61.0 jit_solution(6544154531637089423)
XLA Ops:
  0.0 59.3 %shard_map.82 = bf16[2,64,768]{2,1,0:T(8,128)(2,1)} custom-call(bf16[2,64,768]{2,1,0:T(8,128)(2,1)} %tok_hbm.1, s32[2,2,64]{2,1,0:T(2,128)} %bitcast.17, s32[2,2,64]{2,1,0:T(2,128)} %bitcast.18, f32[2,2,64]{2,1,0:T(2,128)} %bitcast.19, f32[1,768]{1,0:T(1,128)} %gain_hbm.1, bf16[768,3072]{1,0:T(8,128)(2,1)} %bitcast.13, bf16[768,3072]{1,0:T(8,128)(2,1)} %bitcast.14, ...), custom_call_target="tpu_custom_call" | custom-call | tf_op jit(solution)/shard_map/pallas_call | solution.py:450
  59.3 1.6 %copy.10 = bf16[1,2,64,768]{3,2,1,0:T(8,128)(2,1)} copy(bf16[1,2,64,768]{3,2,1,0:T(8,128)(2,1)} %bitcast.16) | data formatting | bytes 393216

commit v2 on v1

--- a/solution.py
+++ b/solution.py
@@ -18,9 +18,9 @@
     out_ref,
     tok, ids, slots, gates, gain, held, packed, relay, arrived, answer, parts, summed, back,
     hits, hits_t, first_t, meta_out, meta_z, meta_in, pick, pick_t, pick_w,
-    xs, inner, scaled, wg, wu, wd,
+    xs, inner, lead, scaled, wg, wu, wd,
     in_sem, w_sem, first_send, first_recv, mz_send, mz_recv, mo_send, mo_recv, mf_send, mf_recv,
-    z_send, z_recv, own_send, own_recv, fan_send, fan_recv, part_send, part_recv,
+    z_send, z_recv, own_send, own_recv, fan_send, fan_recv, part_send, part_recv, twin_recv,
     back_send, back_recv, relay_send, relay_recv,
 ):
     n_node, n_local, micro, toks, width, cap, limit, chunks, ff_chunks = sizes
@@ -44,7 +44,11 @@
         return j
 
     others = [near(k) for k in range(1, n_node)]
+    across = n_local - 1 - local
     plane = [lax.rem(local + i, n_local) for i in range(1, n_local)]
+    if n_local == 4:
+        beside = local + 1 - 2 * lax.rem(local, 2)
+        plane = [across, beside, n_local - 1 - beside]
 
     def remote(src, dst, send, recv, **to):
         return pltpu.make_async_remote_copy(
@@ -86,10 +90,8 @@
         pltpu.make_async_copy(src, dst, w_sem.at[i])
         for i, (src, dst) in enumerate(((wg_hbm, wg), (wu_hbm, wu), (wd_hbm, wd)))
     ]
-    for load in loads:
+    for load in loads[:3]:
         load.wait()
-    for copy in weights_in:
-        copy.start()
 
     slot_span = lax.broadcasted_iota(jnp.int32, (n_node * cap, toks), 0)
     for mb in range(micro):
@@ -129,6 +131,12 @@
                 ]
         meta_in[me] = meta_out[node]
 
+    note_weights()
+    for load in loads[3:]:
+        load.wait()
+    for copy in weights_in:
+        copy.start()
+
     def pack(mb, h):
         floats = h.astype(jnp.float32)
         mean_square = jnp.mean(floats * floats, axis=-1, keepdims=True)
@@ -154,32 +162,38 @@
             jnp.int32, (total, total), 1
         )
         upto = jnp.where(upto, 1.0, 0.0).astype(half)
-        spot = lax.broadcasted_iota(jnp.int32, (limit, total), 0).astype(jnp.float32)
+        down_span = lax.broadcasted_iota(jnp.int32, (limit, total), 0).astype(jnp.float32)
+        over_span = lax.broadcasted_iota(jnp.int32, (total, limit), 1).astype(jnp.float32)
         per_group = LANES // cap
+        w_rows = []
         for mb in range(micro):
             mine = pl.ds(mb * n_local + local, 1)
-            w_row = jnp.concatenate(
-                [
-                    sum(meta_in[g * per_group + b, mine, :] for b in range(per_group))
-                    for g in range(total // LANES)
-                ],
-                axis=1,
+            w_rows.append(
+                jnp.concatenate(
+                    [
+                        sum(meta_in[g * per_group + b, mine, :] for b in range(per_group))
+                        for g in range(total // LANES)
+                    ],
+                    axis=1,
+                )
             )
-            w_rows = jnp.broadcast_to(w_row, (8, total))
-            chosen = jnp.where(w_rows > 0.0, 1.0, 0.0)
-            rank = jnp.dot(chosen.astype(half), upto, preferred_element_type=jnp.float32)
-            rank = jnp.where(w_rows > 0.0, rank - 1.0, -1.0)
-            is_at = spot == jnp.broadcast_to(rank[0:1], (limit, total))
-            place = jnp.where(is_at, 1.0, 0.0)
-            pick[mb] = place.astype(half)
-            pick_t[mb] = place.T.astype(half)
+        w_all = jnp.concatenate(w_rows + [jnp.zeros((8 - micro, total), jnp.float32)], axis=0)
+        chosen = jnp.where(w_all > 0.0, 1.0, 0.0)
+        rank = jnp.dot(chosen.astype(half), upto, preferred_element_type=jnp.float32)
+        rank = jnp.where(w_all > 0.0, rank - 1.0, -1.0)
+        rank_t = rank.T
+        for mb in range(micro):
+            is_at = down_span == jnp.broadcast_to(rank[mb : mb + 1], (limit, total))
+            pick[mb] = jnp.where(is_at, 1.0, 0.0).astype(half)
+            put_at = over_span == jnp.broadcast_to(rank_t[:, mb : mb + 1], (total, limit))
+            pick_t[mb] = jnp.where(put_at, 1.0, 0.0).astype(half)
             pick_w[mb] = jnp.sum(
-                jnp.where(is_at, jnp.broadcast_to(w_row, (limit, total)), 0.0),
+                jnp.where(is_at, jnp.broadcast_to(w_rows[mb], (limit, total)), 0.0),
                 axis=1, keepdims=True,
             )
 
-    def hand_second(mb):
-        for j in others:
+    def hand_second(mb, nodes):
+        for j in nodes:
             block = arrived.at[mb, local, j]
             got(block, z_recv.at[1, mb, j])
             for i in plane:
@@ -207,51 +221,89 @@
             for copy in weights_in:
                 copy.wait()
 
-        with NS("up"):
-            for f in range(ff_chunks):
-                cols = slice(f * fw, (f + 1) * fw)
-                x = xs[...]
-                gate = jnp.dot(x, wg[:, cols], preferred_element_type=jnp.float32)
-                up = jnp.dot(x, wu[:, cols], preferred_element_type=jnp.float32)
-                inner[:, cols] = (jax.nn.gelu(gate, approximate=True) * up).astype(half)
-                if f == ff_chunks // 3 - 1:
-
-                    @pl.when(jnp.logical_and(sec == 1, mb + 1 < micro))
-                    def _():
-                        hand_second(mb + 1)
+        def rise(between):
+            with NS("up"):
+                for f in range(ff_chunks):
+                    cols = slice(f * fw, (f + 1) * fw)
+                    x = xs[...]
+                    gate = jnp.dot(x, wg[:, cols], preferred_element_type=jnp.float32)
+                    up = jnp.dot(x, wu[:, cols], preferred_element_type=jnp.float32)
+                    act = (jax.nn.gelu(gate, approximate=True) * up).astype(half)
+                    inner[:, cols] = act
+                    if f > 0:
+                        prior = slice((f - 1) * fw, f * fw)
+                        part = jnp.dot(
+                            inner[:, prior], wd[prior, :cw], preferred_element_type=jnp.float32
+                        )
+                        lead[...] = part if f == 1 else lead[...] + part
+                    between(f)
+                last = slice((ff_chunks - 1) * fw, ff_chunks * fw)
+                lead[...] += jnp.dot(
+                    inner[:, last], wd[last, :cw], preferred_element_type=jnp.float32
+                )
+
+        def hand_next(f):
+            done = f + 1
+            if done * 3 % ff_chunks == 0:
+                third = done * 3 // ff_chunks - 1
+                cuts = [0, 1, 2, n_node - 1]
+                hand_second(mb + 1, others[cuts[third] : cuts[third + 1]])
+
+        busy = jnp.logical_and(sec == 1, mb + 1 < micro)
+
+        @pl.when(busy)
+        def _():
+            rise(hand_next)
+
+        @pl.when(jnp.logical_not(busy))
+        def _():
+            rise(lambda f: None)
 
         def down(c):
-            acc = jnp.dot(
-                inner[...], wd[:, c * cw : (c + 1) * cw], preferred_element_type=jnp.float32
-            )
+            acc = lead[...]
+            if c > 0:
+                acc = jnp.dot(
+                    inner[...], wd[:, c * cw : (c + 1) * cw], preferred_element_type=jnp.float32
+                )
             scaled[c] = (pick_w[mb] * acc).astype(half)
+
+        def lay(c):
+            spread = jnp.dot(pick_t[mb], scaled[c], preferred_element_type=jnp.float32)
+            answer[mb, c] = spread.reshape(n_local, n_node, cap, cw).astype(half)
+
+        def send(c):
+            for i in plane:
+                remote(
+                    answer.at[mb, c, i], parts.at[sec, mb, c, local],
+                    part_send.at[mb], part_recv.at[sec, mb, c], section=1, local=i,
+                ).start()
 
         with NS("down"):
             down(0)
-            for c in range(chunks):
-                if c + 1 < chunks:
-                    down(c + 1)
-                spread = jnp.dot(pick_t[mb], scaled[c], preferred_element_type=jnp.float32)
-                answer[mb, c] = spread.reshape(n_local, n_node, cap, cw).astype(half)
-                for i in plane:
-                    remote(
-                        answer.at[mb, c, i], parts.at[sec, mb, c, local],
-                        part_send.at[mb], part_recv.at[sec, mb, c], section=1, local=i,
-                    ).start()
+            lay(0)
+            send(0)
+            for c in range(1, chunks):
+                down(c)
+                if c > 1:
+                    lay(c - 1)
+            lay(chunks - 1)
+            for c in range(1, chunks):
+                send(c)
 
         @pl.when(sec == 0)
         def _():
-            for c in range(chunks):
-                remote(
-                    answer.at[mb, c, local], parts.at[0, mb, c, local],
-                    part_send.at[mb], part_recv.at[0, mb, c], section=1,
-                ).start()
+            remote(
+                answer.at[mb, :, local], parts.at[0, mb, :, local],
+                part_send.at[mb], twin_recv.at[mb], section=1,
+            ).start()
 
         return carry
 
     def collect(layer, mb, c):
         if layer == 0:
-            got(parts.at[0, mb, c], part_recv.at[0, mb, c])
+            got(parts.at[0, mb, c, pl.ds(0, n_local - 1)], part_recv.at[0, mb, c])
+            if c == 0:
+                got(parts.at[0, mb, :, local], twin_recv.at[mb])
             rows = sum(parts[0, mb, c, i].astype(jnp.float32) for i in range(n_local))
         else:
             got(parts.at[1, mb, c, pl.ds(0, n_local - 1)], part_recv.at[1, mb, c])
@@ -259,7 +311,7 @@
             for i in plane:
                 rows = rows + parts[1, mb, c, i].astype(jnp.float32)
         summed[layer, mb, c] = rows.astype(half)
-        for j in others:
+        for j in others[::-1]:
             remote(
                 summed.at[layer, mb, c, j], back.at[layer, mb, c, node],
                 back_send.at[layer, mb], back_recv.at[layer, mb, c], node=j,
@@ -289,13 +341,12 @@
                     z_recv.at[0, mb, node], section=1, node=j,
                 ).start()
 
-        z_out(0)
-        own_fan(0, own_recv.at[0])
-        note_weights()
-        for j in others:
+        for j in others[::-1]:
             remote(
                 meta_out.at[j], meta_z.at[node], mz_send, mz_recv.at[0, node], section=1, node=j
             ).start()
+        z_out(0)
+        own_fan(0, own_recv.at[0])
         for i in plane:
             remote(meta_out.at[node], meta_in.at[me], mo_send, mo_recv, local=i).start()
         for mb in range(1, micro):
@@ -323,19 +374,17 @@
                         fan_send.at[0, mb], fan_recv.at[mb], section=0, local=i,
                     ).start()
 
-        note_weights()
         with NS("hand0"):
-            hand_first(0, others[:-1])
-        with NS("relaymeta"):
-            for j in others:
+            for k, j in enumerate(others):
                 got(meta_z.at[j], mz_recv.at[0, j])
                 for i in plane + [local]:
                     remote(
                         meta_z.at[j], meta_in.at[local * n_node + j], mf_send.at[0], mf_recv,
                         section=0, local=i,
                     ).start()
-        with NS("hand0b"):
-            hand_first(0, others[-1:])
+                if k == 0:
+                    hand_first(0, [j])
+            hand_first(0, others[1:])
         for j in others:
             remote(
                 meta_out.at[j], meta_in.at[me], mz_send, mz_recv.at[1, node], node=j
@@ -381,7 +430,7 @@
                     collect(0, mb, c)
             if mb == 1:
                 with NS("second0"):
-                    hand_second(0)
+                    hand_second(0, others)
             with NS(f"combine0{mb}"):
                 combine(0, mb, tok, held)
             dispatch(mb)
@@ -449,7 +498,7 @@
         mem = pltpu.VMEM
         out = pl.pallas_call(
             functools.partial(relay_kernel, sizes),
-            out_shape=jax.ShapeDtypeStruct((micro, toks, width), half),
+            out_shape=pltpu.VMEM((micro, toks, width), half),
             in_specs=[hbm] * 8,
             out_specs=vmem,
             scratch_shapes=[
@@ -477,6 +526,7 @@
                 mem((micro, limit, 1), full),
                 mem((limit, width), half),
                 mem((limit, hidden), half),
+                mem((limit, cw), full),
                 mem((chunks, limit, cw), half),
                 mem((width, hidden), half),
                 mem((width, hidden), half),
@@ -486,7 +536,7 @@
                 dma(()), dma((2, n_node)), dma(()), dma(()), dma((2,)), dma(()),
                 dma((micro,)), dma((2, micro, n_node)), dma((micro,)), dma((micro,)),
                 dma((2, micro)), dma((micro,)),
-                dma((micro,)), dma((2, micro, chunks)),
+                dma((micro,)), dma((2, micro, chunks)), dma((micro,)),
                 dma((2, micro)), dma((2, micro, chunks)),
                 dma((micro,)), dma((micro,)),
             ],

time: 61.1 us -> 56.5 us (0.925)
  Pallas kernels: 59.3 us -> 55.7 us
  local copies, waits for them, and re-layouts: 1.62 us -> 0.68 us
    pallas_call x1, Pallas kernels: 59.3 us -> 55.7 us  [on_device(): pl.pallas_call(functools.partial(relay_kernel, sizes), out_shape=pltpu.VM...]
    unnamed x1, local copies, waits for them, and re-layouts: 1.62 us -> 0.68 us
where the time goes in v2:
time: 56.5 us; the launch traced here: 56.4 us
  Pallas kernels  55.7 us (99%)
  local copies, waits for them, and re-layouts  0.68 us (1%)
    pallas_call x1, Pallas kernels, on_device(): pl.pallas_call(functools.partial(relay_kernel, sizes), out_shape=pltpu.VM...  55.7 us

profile of v2, /device:TPU:1, one launch (start us, length us, event | category | flops | bytes accessed | tf_op | source)
XLA Modules:
  0.0 56.4 jit_solution(18001057264804071113)
XLA Ops:
  0.0 55.7 %shard_map.82 = bf16[2,64,768]{2,1,0:T(8,128)(2,1)S(1)} custom-call(bf16[2,64,768]{2,1,0:T(8,128)(2,1)} %tok_hbm.1, s32[2,2,64]{2,1,0:T(2,128)} %bitcast.17, s32[2,2,64]{2,1,0:T(2,128)} %bitcast.18, f32[2,2,64]{2,1,0:T(2,128)} %bitcast.19, f32[1,768]{1,0:T(1,128)} %gain_hbm.1, bf16[768,3072]{1,0:T(8,128)(2,1)} %bitcast.14, bf16[768,3072]{1,0:T(8,128)(2,1)} %bitcast.15, ...), custom_call_target="tpu_custom_call" | custom-call | tf_op jit(solution)/shard_map/pallas_call | solution.py:499
  55.7 0.7 %copy.10 = bf16[1,2,64,768]{3,2,1,0:T(8,128)(2,1)} copy(bf16[1,2,64,768]{3,2,1,0:T(8,128)(2,1)S(1)} %bitcast.13) | data formatting | bytes 393216

commit v3 on v2

--- a/solution.py
+++ b/solution.py
@@ -26,13 +26,19 @@
     n_node, n_local, micro, toks, width, cap, limit, chunks, ff_chunks = sizes
     n = n_node * n_local
     total = n * cap
+    assert n_node * cap == LANES and n_local == 4 and limit == 2 * LANES
     cw = width // chunks
     fw = inner.shape[1] // ff_chunks
     half = jnp.bfloat16
     sec = lax.axis_index("section")
     node = lax.axis_index("node")
     local = lax.axis_index("local")
-    me = local * n_node + node
+    mid = limit // 2
+
+    def turn(i):
+        return lax.rem(local + i + 1, n_local)
+
+    mine = turn(local)
 
     def near(k):
         if n_node != 4:
@@ -45,7 +51,7 @@
 
     others = [near(k) for k in range(1, n_node)]
     across = n_local - 1 - local
-    plane = [lax.rem(local + i, n_local) for i in range(1, n_local)]
+    plane = [across] + [lax.rem(across + i, n_local) for i in range(1, n_local)]
     if n_local == 4:
         beside = local + 1 - 2 * lax.rem(local, 2)
         plane = [across, beside, n_local - 1 - beside]
@@ -108,7 +114,7 @@
     def note_weights():
         exp_span = lax.broadcasted_iota(jnp.int32, (n, toks), 0)
         lane_span = lax.broadcasted_iota(jnp.int32, (LANES, toks), 0)
-        my_lane = lax.rem(me * cap, LANES)
+        my_lane = node * cap
         for mb in range(micro):
             named = []
             lanes = []
@@ -129,7 +135,7 @@
                 meta_out[j, mb * n_local : (mb + 1) * n_local] = weights[
                     j * n_local : (j + 1) * n_local
                 ]
-        meta_in[me] = meta_out[node]
+        meta_in[mine * n_node + node] = meta_out[node]
 
     note_weights()
     for load in loads[3:]:
@@ -144,12 +150,12 @@
         rows = jnp.dot(hits[mb], normed, preferred_element_type=jnp.float32)
         for j in range(n_node):
             packed[mb, j] = rows[j * cap : (j + 1) * cap].astype(half)
-        arrived[mb, local, node] = packed[mb, node]
+        arrived[mb, mine, node] = packed[mb, node]
 
     def own_fan(mb, recv):
         for i in plane:
             remote(
-                packed.at[mb, node], arrived.at[mb, local, node], own_send.at[mb], recv, local=i
+                packed.at[mb, node], arrived.at[mb, turn(i), node], own_send.at[mb], recv, local=i
             ).start()
 
     def flat(blocks):
@@ -167,11 +173,11 @@
         per_group = LANES // cap
         w_rows = []
         for mb in range(micro):
-            mine = pl.ds(mb * n_local + local, 1)
+            row = pl.ds(mb * n_local + local, 1)
             w_rows.append(
                 jnp.concatenate(
                     [
-                        sum(meta_in[g * per_group + b, mine, :] for b in range(per_group))
+                        sum(meta_in[g * per_group + b, row, :] for b in range(per_group))
                         for g in range(total // LANES)
                     ],
                     axis=1,
@@ -194,110 +200,12 @@
 
     def hand_second(mb, nodes):
         for j in nodes:
-            block = arrived.at[mb, local, j]
+            block = arrived.at[mb, mine, j]
             got(block, z_recv.at[1, mb, j])
             for i in plane:
-                remote(block, block, fan_send.at[1, mb], fan_recv.at[mb], local=i).start()
-
-    def expert(mb, carry):
-        @pl.when(sec == 0)
-        def _():
-            with NS("fan"):
-                got(arrived.at[mb, pl.ds(0, n_local - 1), 0], own_recv.at[mb])
-                got(arrived.at[mb, :, pl.ds(0, n_node - 1)], fan_recv.at[mb])
-
-        @pl.when(sec == 1)
-        def _():
-            with NS("fan"):
-                got(arrived.at[mb, pl.ds(0, n_local - 1)], fan_recv.at[mb])
-
-        with NS("pick"):
-            xs[...] = jnp.dot(
-                pick[mb], flat(arrived[mb]), preferred_element_type=jnp.float32
-            ).astype(half)
-
-        @pl.when(mb == 0)
-        def _():
-            for copy in weights_in:
-                copy.wait()
-
-        def rise(between):
-            with NS("up"):
-                for f in range(ff_chunks):
-                    cols = slice(f * fw, (f + 1) * fw)
-                    x = xs[...]
-                    gate = jnp.dot(x, wg[:, cols], preferred_element_type=jnp.float32)
-                    up = jnp.dot(x, wu[:, cols], preferred_element_type=jnp.float32)
-                    act = (jax.nn.gelu(gate, approximate=True) * up).astype(half)
-                    inner[:, cols] = act
-                    if f > 0:
-                        prior = slice((f - 1) * fw, f * fw)
-                        part = jnp.dot(
-                            inner[:, prior], wd[prior, :cw], preferred_element_type=jnp.float32
-                        )
-                        lead[...] = part if f == 1 else lead[...] + part
-                    between(f)
-                last = slice((ff_chunks - 1) * fw, ff_chunks * fw)
-                lead[...] += jnp.dot(
-                    inner[:, last], wd[last, :cw], preferred_element_type=jnp.float32
-                )
-
-        def hand_next(f):
-            done = f + 1
-            if done * 3 % ff_chunks == 0:
-                third = done * 3 // ff_chunks - 1
-                cuts = [0, 1, 2, n_node - 1]
-                hand_second(mb + 1, others[cuts[third] : cuts[third + 1]])
-
-        busy = jnp.logical_and(sec == 1, mb + 1 < micro)
-
-        @pl.when(busy)
-        def _():
-            rise(hand_next)
-
-        @pl.when(jnp.logical_not(busy))
-        def _():
-            rise(lambda f: None)
-
-        def down(c):
-            acc = lead[...]
-            if c > 0:
-                acc = jnp.dot(
-                    inner[...], wd[:, c * cw : (c + 1) * cw], preferred_element_type=jnp.float32
-                )
-            scaled[c] = (pick_w[mb] * acc).astype(half)
-
-        def lay(c):
-            spread = jnp.dot(pick_t[mb], scaled[c], preferred_element_type=jnp.float32)
-            answer[mb, c] = spread.reshape(n_local, n_node, cap, cw).astype(half)
-
-        def send(c):
-            for i in plane:
                 remote(
-                    answer.at[mb, c, i], parts.at[sec, mb, c, local],
-                    part_send.at[mb], part_recv.at[sec, mb, c], section=1, local=i,
+                    block, arrived.at[mb, turn(i), j], fan_send.at[1, mb], fan_recv.at[mb], local=i
                 ).start()
-
-        with NS("down"):
-            down(0)
-            lay(0)
-            send(0)
-            for c in range(1, chunks):
-                down(c)
-                if c > 1:
-                    lay(c - 1)
-            lay(chunks - 1)
-            for c in range(1, chunks):
-                send(c)
-
-        @pl.when(sec == 0)
-        def _():
-            remote(
-                answer.at[mb, :, local], parts.at[0, mb, :, local],
-                part_send.at[mb], twin_recv.at[mb], section=1,
-            ).start()
-
-        return carry
 
     def collect(layer, mb, c):
         if layer == 0:
@@ -307,7 +215,7 @@
             rows = sum(parts[0, mb, c, i].astype(jnp.float32) for i in range(n_local))
         else:
             got(parts.at[1, mb, c, pl.ds(0, n_local - 1)], part_recv.at[1, mb, c])
-            rows = answer[mb, c, local].astype(jnp.float32)
+            rows = answer[mb, c, mine].astype(jnp.float32)
             for i in plane:
                 rows = rows + parts[1, mb, c, i].astype(jnp.float32)
         summed[layer, mb, c] = rows.astype(half)
@@ -317,6 +225,131 @@
                 back_send.at[layer, mb], back_recv.at[layer, mb, c], node=j,
             ).start()
         back[layer, mb, c, node] = summed[layer, mb, c, node]
+
+    def expert(mb, carry):
+        @pl.when(sec == 0)
+        def _():
+            with NS("fan"):
+                got(arrived.at[mb, pl.ds(0, n_local - 1), 0], own_recv.at[mb])
+                got(arrived.at[mb, :, pl.ds(0, n_node - 1)], fan_recv.at[mb])
+
+        @pl.when(sec == 1)
+        def _():
+            with NS("fan"):
+                got(arrived.at[mb, pl.ds(0, n_local - 1)], fan_recv.at[mb])
+
+        @pl.when(mb == 0)
+        def _():
+            for copy in weights_in:
+                copy.wait()
+
+        def send(c, i):
+            remote(
+                answer.at[mb, c, turn(i)], parts.at[sec, mb, c, local],
+                part_send.at[mb], part_recv.at[sec, mb, c], section=1, local=i,
+            ).start()
+
+        def rise(rows, leading, between):
+            xs[rows] = jnp.dot(
+                pick[mb, rows], flat(arrived[mb]), preferred_element_type=jnp.float32
+            ).astype(half)
+            for f in range(ff_chunks):
+                cols = slice(f * fw, (f + 1) * fw)
+                x = xs[rows]
+                gate = jnp.dot(x, wg[:, cols], preferred_element_type=jnp.float32)
+                up = jnp.dot(x, wu[:, cols], preferred_element_type=jnp.float32)
+                inner[rows, cols] = (jax.nn.gelu(gate, approximate=True) * up).astype(half)
+                if leading and f > 0:
+                    prior = slice((f - 1) * fw, f * fw)
+                    part = jnp.dot(
+                        inner[rows, prior], wd[prior, :cw], preferred_element_type=jnp.float32
+                    )
+                    lead[rows] = part if f == 1 else lead[rows] + part
+                between(f)
+            if leading:
+                last = slice((ff_chunks - 1) * fw, ff_chunks * fw)
+                lead[rows] += jnp.dot(
+                    inner[rows, last], wd[last, :cw], preferred_element_type=jnp.float32
+                )
+
+        def down(c, rows, acc=None):
+            if acc is None:
+                acc = jnp.dot(
+                    inner[rows], wd[:, c * cw : (c + 1) * cw], preferred_element_type=jnp.float32
+                )
+            scaled[c, rows] = (pick_w[mb, rows] * acc).astype(half)
+
+        def lay(c, first, count, depth):
+            span = n_node * cap
+            spread = jnp.dot(
+                pick_t[mb, first * span : (first + count) * span, :depth], scaled[c, :depth],
+                preferred_element_type=jnp.float32,
+            )
+            answer[mb, c, first : first + count] = spread.reshape(
+                count, n_node, cap, cw
+            ).astype(half)
+
+        whole, top, low = slice(0, limit), slice(0, mid), slice(mid, limit)
+
+        def finish(rows, first, targets):
+            down(0, rows, lead[rows])
+            lay(0, first, n_local - first, limit)
+            for i in targets:
+                send(0, i)
+            for c in range(1, chunks):
+                down(c, rows)
+                if c > 1:
+                    lay(c - 1, first, n_local - first, limit)
+            lay(chunks - 1, first, n_local - first, limit)
+            for c in range(1, chunks):
+                for i in targets:
+                    send(c, i)
+
+        def hand_next(f):
+            if done_at(f):
+                hand_second(mb + 1, others[f * 3 // ff_chunks : f * 3 // ff_chunks + 1])
+                if f == ff_chunks - 1:
+                    hand_second(mb + 1, others[3:])
+
+        def done_at(f):
+            return (f + 1) * 3 % ff_chunks == 0
+
+        def collect_prior(f):
+            stops = [ff_chunks - 1, ff_chunks + 1, 2 * ff_chunks - 1]
+            if micro > 1 and f in stops:
+                collect(1, micro - 2, stops.index(f))
+
+        @pl.when(jnp.logical_and(sec == 1, mb < micro - 1))
+        def _():
+            rise(whole, True, hand_next)
+            finish(whole, 0, plane)
+
+        @pl.when(jnp.logical_and(sec == 1, mb == micro - 1))
+        def _():
+            rise(top, False, collect_prior)
+            down(0, top)
+            for c in range(1, chunks):
+                down(c, top)
+                lay(c - 1, 0, 1, mid)
+            lay(chunks - 1, 0, 1, mid)
+            for c in range(chunks):
+                send(c, plane[0])
+            rise(low, True, lambda f: collect_prior(ff_chunks + f))
+            finish(low, 1, plane[1:])
+
+        @pl.when(sec == 0)
+        def _():
+            rise(whole, True, lambda f: None)
+            finish(whole, 0, plane)
+
+        @pl.when(sec == 0)
+        def _():
+            remote(
+                answer.at[mb, :, mine], parts.at[0, mb, :, local],
+                part_send.at[mb], twin_recv.at[mb], section=1,
+            ).start()
+
+        return carry
 
     def combine(layer, mb, base, where):
         for c in range(chunks):
@@ -348,7 +381,9 @@
         z_out(0)
         own_fan(0, own_recv.at[0])
         for i in plane:
-            remote(meta_out.at[node], meta_in.at[me], mo_send, mo_recv, local=i).start()
+            remote(
+                meta_out.at[node], meta_in.at[turn(i) * n_node + node], mo_send, mo_recv, local=i
+            ).start()
         for mb in range(1, micro):
             pack(mb, tok[mb])
             z_out(mb)
@@ -370,7 +405,7 @@
                 got(relay.at[mb, j], z_recv.at[0, mb, j])
                 for i in plane + [local]:
                     remote(
-                        relay.at[mb, j], arrived.at[mb, local, j],
+                        relay.at[mb, j], arrived.at[mb, turn(i), j],
                         fan_send.at[0, mb], fan_recv.at[mb], section=0, local=i,
                     ).start()
 
@@ -379,7 +414,7 @@
                 got(meta_z.at[j], mz_recv.at[0, j])
                 for i in plane + [local]:
                     remote(
-                        meta_z.at[j], meta_in.at[local * n_node + j], mf_send.at[0], mf_recv,
+                        meta_z.at[j], meta_in.at[turn(i) * n_node + j], mf_send.at[0], mf_recv,
                         section=0, local=i,
                     ).start()
                 if k == 0:
@@ -387,19 +422,24 @@
             hand_first(0, others[1:])
         for j in others:
             remote(
-                meta_out.at[j], meta_in.at[me], mz_send, mz_recv.at[1, node], node=j
+                meta_out.at[j], meta_in.at[mine * n_node + node], mz_send,
+                mz_recv.at[1, node], node=j,
             ).start()
         for i in plane:
-            remote(meta_out.at[node], meta_in.at[me], mo_send, mo_recv, local=i).start()
+            remote(
+                meta_out.at[node], meta_in.at[turn(i) * n_node + node], mo_send, mo_recv, local=i
+            ).start()
         for mb in range(1, micro):
             with NS(f"hand{mb}"):
                 hand_first(mb, others)
         with NS("handm"):
             for j in others:
-                block = meta_in.at[local * n_node + j]
+                block = meta_in.at[mine * n_node + j]
                 got(block, mz_recv.at[1, j])
                 for i in plane:
-                    remote(block, block, mf_send.at[1], mf_recv, local=i).start()
+                    remote(
+                        block, meta_in.at[turn(i) * n_node + j], mf_send.at[1], mf_recv, local=i
+                    ).start()
         with NS("metawait"):
             got(meta_in.at[pl.ds(0, n_local - 1)], mo_recv)
             got(meta_in.at[pl.ds(0, (n_node - 1) * (n_local - 1))], mf_recv)
@@ -410,7 +450,7 @@
             pack(mb, held[mb])
             for j in others:
                 remote(
-                    packed.at[mb, j], arrived.at[mb, local, node], z_send.at[mb],
+                    packed.at[mb, j], arrived.at[mb, mine, node], z_send.at[mb],
                     z_recv.at[1, mb, node], node=j,
                 ).start()
             own_fan(mb, fan_recv.at[mb])
@@ -453,10 +493,9 @@
 
     @pl.when(sec == 1)
     def _():
-        for mb in range(micro):
-            with NS(f"collect1{mb}"):
-                for c in range(chunks):
-                    collect(1, mb, c)
+        with NS("collect11"):
+            for c in range(chunks):
+                collect(1, micro - 1, c)
         for mb in range(micro):
             with NS(f"combine1{mb}"):
                 combine(1, mb, held, out_ref)

time: 56.5 us -> 55.4 us (0.981)
  Pallas kernels: 55.7 us -> 54.6 us
    pallas_call x1, Pallas kernels: 55.7 us -> 54.6 us  [on_device(): pl.pallas_call(functools.partial(relay_kernel, sizes), out_shape=pltpu.VM...]
where the time goes in v3:
time: 55.4 us; the launch traced here: 55.3 us
  Pallas kernels  54.6 us (99%)
  local copies, waits for them, and re-layouts  0.68 us (1%)
    pallas_call x1, Pallas kernels, on_device(): pl.pallas_call(functools.partial(relay_kernel, sizes), out_shape=pltpu.VM...  54.6 us

profile of v3, /device:TPU:1, one launch (start us, length us, event | category | flops | bytes accessed | tf_op | source)
XLA Modules:
  0.0 55.3 jit_solution(15126299194938597523)
XLA Ops:
  0.0 54.6 %shard_map.82 = bf16[2,64,768]{2,1,0:T(8,128)(2,1)S(1)} custom-call(bf16[2,64,768]{2,1,0:T(8,128)(2,1)} %tok_hbm.1, s32[2,2,64]{2,1,0:T(2,128)} %bitcast.17, s32[2,2,64]{2,1,0:T(2,128)} %bitcast.18, f32[2,2,64]{2,1,0:T(2,128)} %bitcast.19, f32[1,768]{1,0:T(1,128)} %gain_hbm.1, bf16[768,3072]{1,0:T(8,128)(2,1)} %bitcast.14, bf16[768,3072]{1,0:T(8,128)(2,1)} %bitcast.15, ...), custom_call_target="tpu_custom_call" | custom-call | tf_op jit(solution)/shard_map/pallas_call | solution.py:538
  54.6 0.7 %copy.10 = bf16[1,2,64,768]{3,2,1,0:T(8,128)(2,1)} copy(bf16[1,2,64,768]{3,2,1,0:T(8,128)(2,1)S(1)} %bitcast.13) | data formatting | bytes 393216

commit v4 on v3

--- a/solution.py
+++ b/solution.py
@@ -19,7 +19,7 @@
     tok, ids, slots, gates, gain, held, packed, relay, arrived, answer, parts, summed, back,
     hits, hits_t, first_t, meta_out, meta_z, meta_in, pick, pick_t, pick_w,
     xs, inner, lead, scaled, wg, wu, wd,
-    in_sem, w_sem, first_send, first_recv, mz_send, mz_recv, mo_send, mo_recv, mf_send, mf_recv,
+    in_sem, w_sem, first_send, first_recv, mz_send, mz_recv, hz_recv, mo_send, mo_recv, mf_send, mf_recv,
     z_send, z_recv, own_send, own_recv, fan_send, fan_recv, part_send, part_recv, twin_recv,
     back_send, back_recv, relay_send, relay_recv,
 ):
@@ -155,7 +155,7 @@
     def own_fan(mb, recv):
         for i in plane:
             remote(
-                packed.at[mb, node], arrived.at[mb, turn(i), node], own_send.at[mb], recv, local=i
+                packed.at[mb, node], arrived.at[mb, turn(i), node], own_send, recv, local=i
             ).start()
 
     def flat(blocks):
@@ -201,20 +201,20 @@
     def hand_second(mb, nodes):
         for j in nodes:
             block = arrived.at[mb, mine, j]
-            got(block, z_recv.at[1, mb, j])
+            got(block, z_recv.at[mb, j])
             for i in plane:
                 remote(
-                    block, arrived.at[mb, turn(i), j], fan_send.at[1, mb], fan_recv.at[mb], local=i
+                    block, arrived.at[mb, turn(i), j], fan_send.at[1], fan_recv.at[mb], local=i
                 ).start()
 
     def collect(layer, mb, c):
         if layer == 0:
-            got(parts.at[0, mb, c, pl.ds(0, n_local - 1)], part_recv.at[0, mb, c])
+            got(parts.at[0, mb, c, pl.ds(0, n_local - 1)], part_recv.at[mb, c])
             if c == 0:
                 got(parts.at[0, mb, :, local], twin_recv.at[mb])
             rows = sum(parts[0, mb, c, i].astype(jnp.float32) for i in range(n_local))
         else:
-            got(parts.at[1, mb, c, pl.ds(0, n_local - 1)], part_recv.at[1, mb, c])
+            got(parts.at[1, mb, c, pl.ds(0, n_local - 1)], part_recv.at[mb, c])
             rows = answer[mb, c, mine].astype(jnp.float32)
             for i in plane:
                 rows = rows + parts[1, mb, c, i].astype(jnp.float32)
@@ -222,7 +222,7 @@
         for j in others[::-1]:
             remote(
                 summed.at[layer, mb, c, j], back.at[layer, mb, c, node],
-                back_send.at[layer, mb], back_recv.at[layer, mb, c], node=j,
+                back_send, back_recv.at[mb, c], node=j,
             ).start()
         back[layer, mb, c, node] = summed[layer, mb, c, node]
 
@@ -246,7 +246,7 @@
         def send(c, i):
             remote(
                 answer.at[mb, c, turn(i)], parts.at[sec, mb, c, local],
-                part_send.at[mb], part_recv.at[sec, mb, c], section=1, local=i,
+                part_send, part_recv.at[mb, c], section=1, local=i,
             ).start()
 
         def rise(rows, leading, between):
@@ -315,9 +315,9 @@
             return (f + 1) * 3 % ff_chunks == 0
 
         def collect_prior(f):
-            stops = [ff_chunks - 1, ff_chunks + 1, 2 * ff_chunks - 1]
-            if micro > 1 and f in stops:
-                collect(1, micro - 2, stops.index(f))
+            if micro > 1 and f == 2 * ff_chunks - 1:
+                for c in range(chunks):
+                    collect(1, micro - 2, c)
 
         @pl.when(jnp.logical_and(sec == 1, mb < micro - 1))
         def _():
@@ -346,14 +346,14 @@
         def _():
             remote(
                 answer.at[mb, :, mine], parts.at[0, mb, :, local],
-                part_send.at[mb], twin_recv.at[mb], section=1,
+                part_send, twin_recv.at[mb], section=1,
             ).start()
 
         return carry
 
     def combine(layer, mb, base, where):
         for c in range(chunks):
-            got(back.at[layer, mb, c, pl.ds(0, n_node - 1)], back_recv.at[layer, mb, c])
+            got(back.at[layer, mb, c, pl.ds(0, n_node - 1)], back_recv.at[mb, c])
             mixed = jnp.dot(
                 (first_t if layer == 0 else hits_t)[mb], flat(back[layer, mb, c]),
                 preferred_element_type=jnp.float32,
@@ -370,13 +370,13 @@
         def z_out(mb):
             for j in others:
                 remote(
-                    packed.at[mb, j], relay.at[mb, node], z_send.at[mb],
-                    z_recv.at[0, mb, node], section=1, node=j,
+                    packed.at[mb, j], relay.at[mb, node], z_send,
+                    z_recv.at[mb, node], section=1, node=j,
                 ).start()
 
         for j in others[::-1]:
             remote(
-                meta_out.at[j], meta_z.at[node], mz_send, mz_recv.at[0, node], section=1, node=j
+                meta_out.at[j], meta_z.at[node], mz_send, mz_recv.at[node], section=1, node=j
             ).start()
         z_out(0)
         own_fan(0, own_recv.at[0])
@@ -402,16 +402,16 @@
 
         def hand_first(mb, nodes):
             for j in nodes:
-                got(relay.at[mb, j], z_recv.at[0, mb, j])
+                got(relay.at[mb, j], z_recv.at[mb, j])
                 for i in plane + [local]:
                     remote(
                         relay.at[mb, j], arrived.at[mb, turn(i), j],
-                        fan_send.at[0, mb], fan_recv.at[mb], section=0, local=i,
+                        fan_send.at[0], fan_recv.at[mb], section=0, local=i,
                     ).start()
 
         with NS("hand0"):
             for k, j in enumerate(others):
-                got(meta_z.at[j], mz_recv.at[0, j])
+                got(meta_z.at[j], mz_recv.at[j])
                 for i in plane + [local]:
                     remote(
                         meta_z.at[j], meta_in.at[turn(i) * n_node + j], mf_send.at[0], mf_recv,
@@ -423,7 +423,7 @@
         for j in others:
             remote(
                 meta_out.at[j], meta_in.at[mine * n_node + node], mz_send,
-                mz_recv.at[1, node], node=j,
+                hz_recv, node=j,
             ).start()
         for i in plane:
             remote(
@@ -433,9 +433,9 @@
             with NS(f"hand{mb}"):
                 hand_first(mb, others)
         with NS("handm"):
+            got(meta_in.at[pl.ds(0, n_node - 1)], hz_recv)
             for j in others:
                 block = meta_in.at[mine * n_node + j]
-                got(block, mz_recv.at[1, j])
                 for i in plane:
                     remote(
                         block, meta_in.at[turn(i) * n_node + j], mf_send.at[1], mf_recv, local=i
@@ -450,12 +450,12 @@
             pack(mb, held[mb])
             for j in others:
                 remote(
-                    packed.at[mb, j], arrived.at[mb, mine, node], z_send.at[mb],
-                    z_recv.at[1, mb, node], node=j,
+                    packed.at[mb, j], arrived.at[mb, mine, node], z_send,
+                    z_recv.at[mb, node], node=j,
                 ).start()
             own_fan(mb, fan_recv.at[mb])
             remote(
-                held.at[mb], held.at[mb], relay_send.at[mb], relay_recv.at[mb], section=0
+                held.at[mb], held.at[mb], relay_send, relay_recv.at[mb], section=0
             ).start()
 
         with NS("collect00"):
@@ -486,10 +486,9 @@
         sent(meta_out.at[pl.ds(0, n_node - 1)], mz_send)
         sent(meta_in.at[pl.ds(0, n_local - 1)], mo_send)
         sent(hits_t, first_send)
-        for mb in range(micro):
-            sent(packed.at[mb, pl.ds(0, n_node - 1)], z_send.at[mb])
-            sent(arrived.at[mb, pl.ds(0, n_local - 1), 0], own_send.at[mb])
-            sent(answer.at[mb], part_send.at[mb])
+        sent(packed.at[:, pl.ds(0, n_node - 1)], z_send)
+        sent(arrived.at[:, pl.ds(0, n_local - 1), 0], own_send)
+        sent(answer, part_send)
 
     @pl.when(sec == 1)
     def _():
@@ -504,15 +503,13 @@
             sent(meta_in.at[pl.ds(0, n_local - 1)], mo_send)
             sent(meta_in.at[pl.ds(0, (n_node - 1) * n_local)], mf_send.at[0])
             sent(meta_in.at[pl.ds(0, (n_node - 1) * (n_local - 1))], mf_send.at[1])
-            for mb in range(micro):
-                sent(packed.at[mb, pl.ds(0, n_node - 1)], z_send.at[mb])
-                sent(arrived.at[mb, pl.ds(0, n_local - 1), 0], own_send.at[mb])
-                sent(arrived.at[mb, :, pl.ds(0, n_node - 1)], fan_send.at[0, mb])
-                sent(arrived.at[mb, pl.ds(0, n_local - 1), pl.ds(0, n_node - 1)], fan_send.at[1, mb])
-                sent(answer.at[mb, :, pl.ds(0, n_local - 1)], part_send.at[mb])
-                for layer in range(2):
-                    sent(summed.at[layer, mb, :, pl.ds(0, n_node - 1)], back_send.at[layer, mb])
-                sent(held.at[mb], relay_send.at[mb])
+            sent(packed.at[:, pl.ds(0, n_node - 1)], z_send)
+            sent(arrived.at[:, pl.ds(0, n_local - 1), 0], own_send)
+            sent(arrived.at[:, :, pl.ds(0, n_node - 1)], fan_send.at[0])
+            sent(arrived.at[:, pl.ds(0, n_local - 1), pl.ds(0, n_node - 1)], fan_send.at[1])
+            sent(answer.at[:, :, pl.ds(0, n_local - 1)], part_send)
+            sent(summed.at[:, :, :, pl.ds(0, n_node - 1)], back_send)
+            sent(held, relay_send)
 
 
 def solution(mesh):
@@ -572,12 +569,12 @@
                 mem((hidden, width), half),
                 dma((5,)), dma((3,)),
                 dma(()), dma(()),
-                dma(()), dma((2, n_node)), dma(()), dma(()), dma((2,)), dma(()),
-                dma((micro,)), dma((2, micro, n_node)), dma((micro,)), dma((micro,)),
-                dma((2, micro)), dma((micro,)),
-                dma((micro,)), dma((2, micro, chunks)), dma((micro,)),
-                dma((2, micro)), dma((2, micro, chunks)),
-                dma((micro,)), dma((micro,)),
+                dma(()), dma((n_node,)), dma(()), dma(()), dma(()), dma((2,)), dma(()),
+                dma(()), dma((micro, n_node)), dma(()), dma((micro,)),
+                dma((2,)), dma((micro,)),
+                dma(()), dma((micro, chunks)), dma((micro,)),
+                dma(()), dma((micro, chunks)),
+                dma(()), dma((micro,)),
             ],
             compiler_params=pltpu.CompilerParams(collective_id=0, has_side_effects=True),
         )(

time: 55.4 us -> 54.8 us (0.989)
  Pallas kernels: 54.6 us -> 54 us
    pallas_call x1, Pallas kernels: 54.6 us -> 54 us  [on_device(): pl.pallas_call(functools.partial(relay_kernel, sizes), out_shape=pltpu.VM...]
where the time goes in v4:
time: 54.8 us; the launch traced here: 54.7 us
  Pallas kernels  54 us (99%)
  local copies, waits for them, and re-layouts  0.68 us (1%)
    pallas_call x1, Pallas kernels, on_device(): pl.pallas_call(functools.partial(relay_kernel, sizes), out_shape=pltpu.VM...  54 us

profile of v4, /device:TPU:1, one launch (start us, length us, event | category | flops | bytes accessed | tf_op | source)
XLA Modules:
  0.0 54.7 jit_solution(7496612364458822990)
XLA Ops:
  0.0 54.0 %shard_map.82 = bf16[2,64,768]{2,1,0:T(8,128)(2,1)S(1)} custom-call(bf16[2,64,768]{2,1,0:T(8,128)(2,1)} %tok_hbm.1, s32[2,2,64]{2,1,0:T(2,128)} %bitcast.17, s32[2,2,64]{2,1,0:T(2,128)} %bitcast.18, f32[2,2,64]{2,1,0:T(2,128)} %bitcast.19, f32[1,768]{1,0:T(1,128)} %gain_hbm.1, bf16[768,3072]{1,0:T(8,128)(2,1)} %bitcast.14, bf16[768,3072]{1,0:T(8,128)(2,1)} %bitcast.15, ...), custom_call_target="tpu_custom_call" | custom-call | tf_op jit(solution)/shard_map/pallas_call | solution.py:535
  54.0 0.7 %copy.10 = bf16[1,2,64,768]{3,2,1,0:T(8,128)(2,1)} copy(bf16[1,2,64,768]{3,2,1,0:T(8,128)(2,1)S(1)} %bitcast.13) | data formatting | bytes 393216

commit v5 on v4

--- a/solution.py
+++ b/solution.py
@@ -314,11 +314,6 @@
         def done_at(f):
             return (f + 1) * 3 % ff_chunks == 0
 
-        def collect_prior(f):
-            if micro > 1 and f == 2 * ff_chunks - 1:
-                for c in range(chunks):
-                    collect(1, micro - 2, c)
-
         @pl.when(jnp.logical_and(sec == 1, mb < micro - 1))
         def _():
             rise(whole, True, hand_next)
@@ -326,7 +321,7 @@
 
         @pl.when(jnp.logical_and(sec == 1, mb == micro - 1))
         def _():
-            rise(top, False, collect_prior)
+            rise(top, False, lambda f: None)
             down(0, top)
             for c in range(1, chunks):
                 down(c, top)
@@ -334,7 +329,7 @@
             lay(chunks - 1, 0, 1, mid)
             for c in range(chunks):
                 send(c, plane[0])
-            rise(low, True, lambda f: collect_prior(ff_chunks + f))
+            rise(low, True, lambda f: None)
             finish(low, 1, plane[1:])
 
         @pl.when(sec == 0)
@@ -493,8 +488,9 @@
     @pl.when(sec == 1)
     def _():
         with NS("collect11"):
-            for c in range(chunks):
-                collect(1, micro - 1, c)
+            for mb in range(micro):
+                for c in range(chunks):
+                    collect(1, mb, c)
         for mb in range(micro):
             with NS(f"combine1{mb}"):
                 combine(1, mb, held, out_ref)

time: 54.8 us -> 54.8 us (level)
  no operation moved by 1% of the time
where the time goes in v5:
time: 54.8 us; the launch traced here: 54.6 us
  Pallas kernels  53.9 us (98%)
  local copies, waits for them, and re-layouts  0.68 us (1%)
    pallas_call x1, Pallas kernels, on_device(): pl.pallas_call(functools.partial(relay_kernel, sizes), out_shape=pltpu.VM...  53.9 us

profile of v5, /device:TPU:1, one launch (start us, length us, event | category | flops | bytes accessed | tf_op | source)
XLA Modules:
  0.0 54.6 jit_solution(2236421988198447632)
XLA Ops:
  0.0 53.9 %shard_map.82 = bf16[2,64,768]{2,1,0:T(8,128)(2,1)S(1)} custom-call(bf16[2,64,768]{2,1,0:T(8,128)(2,1)} %tok_hbm.1, s32[2,2,64]{2,1,0:T(2,128)} %bitcast.17, s32[2,2,64]{2,1,0:T(2,128)} %bitcast.18, f32[2,2,64]{2,1,0:T(2,128)} %bitcast.19, f32[1,768]{1,0:T(1,128)} %gain_hbm.1, bf16[768,3072]{1,0:T(8,128)(2,1)} %bitcast.14, bf16[768,3072]{1,0:T(8,128)(2,1)} %bitcast.15, ...), custom_call_target="tpu_custom_call" | custom-call | tf_op jit(solution)/shard_map/pallas_call | solution.py:531
  53.9 0.7 %copy.10 = bf16[1,2,64,768]{3,2,1,0:T(8,128)(2,1)} copy(bf16[1,2,64,768]{3,2,1,0:T(8,128)(2,1)S(1)} %bitcast.13) | data formatting | bytes 393216
